TPU v7x, 32 devices: a 4x4x1 block of a 4x4x8 slice. The times are simulated.
32 devices in a mesh: dp: 1 (over z), ep: 32 (over x, y, core).
Axes of the slice: x: 4, y: 4, z: 1, core: 2. Of those that a mesh axis runs over, the one named last changes fastest.
The devices are a block of a 4x4x8 slice.
Arguments:
- x: bfloat16 [1, 32, 256, 4096], P('dp', 'ep')
- expert: int32 [1, 32, 256, 8], P('dp', 'ep')
- slot: int32 [1, 32, 256, 8], P('dp', 'ep')
- gate: float32 [1, 32, 256, 8], P('dp', 'ep')
- w_gate: bfloat16 [64, 4096, 1536], P('ep')
- w_up: bfloat16 [64, 4096, 1536], P('ep')
- w_down: bfloat16 [64, 1536, 4096], P('ep')
Outputs:
- y: bfloat16 [1, 32, 256, 4096], P('dp', 'ep')
All inputs are finite; a program needn't handle non-finite values.
Results may differ from a plain program's by a relative error of at most 0.009.
Values are sent between devices in bfloat16 or wider.
A program may use at most 768 MiB of HBM per device.

v0:
```python
import jax
import jax.numpy as jnp
from jax import lax
from jax.sharding import NamedSharding, PartitionSpec as P


def einsum(form, a, b):
    return jnp.einsum(form, a.astype(jnp.float32), b.astype(jnp.float32))


def solution(mesh):
    def placed(v, *spec):
        return lax.with_sharding_constraint(v, NamedSharding(mesh, P(*spec)))

    def step(x, expert, slot, gate, w_gate, w_up, w_down):
        experts, (tokens, top) = w_gate.shape[0], expert.shape[2:]
        slots = 5 * tokens * top // (4 * experts)
        to_expert = jax.nn.one_hot(expert, experts, dtype=jnp.bfloat16)
        to_slot = jax.nn.one_hot(slot, slots, dtype=jnp.bfloat16)
        weighted = to_expert * gate[..., None].astype(jnp.bfloat16)
        dispatch = einsum("abtke,abtkc->abtec", to_expert, to_slot).astype(jnp.bfloat16)
        combine = einsum("abtke,abtkc->abtec", weighted, to_slot).astype(jnp.bfloat16)
        z = einsum("abtec,abtd->aebcd", dispatch, x).astype(jnp.bfloat16)
        z = placed(z, "dp", None, "ep", None, None)
        z = placed(z, "dp", "ep", None, None, None)
        h = jax.nn.silu(einsum("aebcd,edf->aebcf", z, w_gate))
        h = (h * einsum("aebcd,edf->aebcf", z, w_up)).astype(jnp.bfloat16)
        out = einsum("aebcf,efd->aebcd", h, w_down).astype(jnp.bfloat16)
        out = placed(out, "dp", "ep", None, None, None)
        out = placed(out, "dp", None, "ep", None, None)
        y = einsum("abtec,aebcd->abtd", combine, out)
        return y.astype(jnp.bfloat16)

    return step
```

profile of v0, /device:TPU:98, one launch (start us, length us, event | category | flops | bytes accessed | tf_op | source)
XLA Modules:
  0.0 723.0 jit_solution(5108111935251248581)
XLA Ops:
  0.0 0.0 copy-start
  0.0 1.0 copy.10
  1.0 0.0 copy-start.2
  1.0 0.8 copy.12
  1.8 0.0 copy-done.2
  1.8 0.0 copy-start.4
  1.9 0.6 copy-done.4
  2.5 3.6 convolution_convert_fusion.1
  6.1 5.6 copy.13
  11.7 0.0 copy-done
  11.8 10.2 %convolution_convert_fusion = bf16[64,40,4096]{2,1,0:T(8,128)(2,1)} fusion(bf16[256,64,40]{0,2,1:T(8,128)(2,1)S(1)} %copy.13, bf16[1,1,256,4096]{3,2,1,0:T(8,128)(2,1)S(1)} %copy-done), kind=kOutput, calls=%fused_computation.18 | convolution fusion | flops 5379194880 | bytes 24379392 | tf_op jit(solution)/abtec,abtd->aebcd/dot_general | solution.py:8
  21.9 259.3 %all-to-all.4 = bf16[1,32,2,1,40,4096]{5,4,2,3,0,1:T(8,128)(2,1)} all-to-all(bf16[1,32,2,1,40,4096]{5,4,2,3,0,1:T(8,128)(2,1)} %bitcast.120), channel_id=1, replica_groups=mesh['dp'=1,'ep'=32] {'ep'}, dimensions={1} | all-to-all | bytes 41943040 | tf_op jit(solution)/sharding_constraint;jit(solution)/sharding_constraint | solution.py:13
  281.2 41.9 %fusion.2 = f32[2,32,40,1536]{3,2,1,0:T(8,128)} fusion(bf16[2,4096,1536]{2,1,0:T(8,128)(2,1)} %param.5, bf16[1,32,2,1,40,4096]{5,4,2,3,0,1:T(8,128)(2,1)} %all-to-all.4), kind=kOutput, calls=%fused_computation.2 | convolution fusion | flops 32212254720 | bytes 61865984 | tf_op jit(solution)/aebcd,edf->aebcf/dot_general | solution.py:8
  323.1 41.8 %fusion.4 = f32[2,32,40,1536]{3,2,1,0:T(8,128)} fusion(bf16[2,4096,1536]{2,1,0:T(8,128)(2,1)} %param.4, bf16[1,32,2,1,40,4096]{5,4,2,3,0,1:T(8,128)(2,1)} %all-to-all.4), kind=kOutput, calls=%fused_computation.4 | convolution fusion | flops 32212254720 | bytes 61865984 | tf_op jit(solution)/aebcd,edf->aebcf/dot_general | solution.py:8
  364.9 46.2 %convert_bitcast_fusion = bf16[1,2,32,1,40,4096]{5,4,2,1,3,0:T(8,128)(2,1)} fusion(bf16[2,1536,4096]{2,1,0:T(8,128)(2,1)} %param.6, f32[2,32,40,1536]{3,2,1,0:T(8,128)} %fusion.2, f32[2,32,40,1536]{3,2,1,0:T(8,128)} %fusion.4), kind=kOutput, calls=%fused_computation.8 | convolution fusion | flops 32246333440 | bytes 77594624 | tf_op jit(solution)/aebcf,efd->aebcd/dot_general | solution.py:8
  411.1 17.5 %copy.16 = bf16[1,2,32,1,40,4096]{5,4,1,3,0,2:T(8,128)(2,1)} copy(bf16[1,2,32,1,40,4096]{5,4,2,1,3,0:T(8,128)(2,1)} %convert_bitcast_fusion) | data formatting | bytes 41943040 | tf_op jit(solution)/sharding_constraint;jit(solution)/sharding_constraint | solution.py:13
  428.6 0.0 copy-start.6
  428.6 0.0 copy-start.3
  428.6 0.0 copy-start.5
  428.6 5.1 all-to-all-start.1
  433.7 0.0 copy-done.6
  433.7 0.1 copy.11
  433.9 0.0 copy-done.3
  433.9 0.0 copy-done.5
  433.9 0.0 copy-start.1
  433.9 4.3 convolution_convert_fusion.2
  438.2 5.6 copy.23
  443.8 267.7 %all-to-all-done.1 = bf16[1,2,32,1,40,4096]{5,4,1,3,0,2:T(8,128)(2,1)} async-done(((bf16[1,2,32,1,40,4096]{5,4,1,3,0,2:T(8,128)(2,1)}), bf16[1,2,32,1,40,4096]{5,4,1,3,0,2:T(8,128)(2,1)}, u32[]{:S(2)}, u32[]{:S(2)}) %all-to-all-start.1) | async-done | bytes 20971552 | tf_op jit(solution)/sharding_constraint;jit(solution)/sharding_constraint | solution.py:13
  711.5 11.5 %fusion.19 = bf16[1,1,256,4096]{3,2,1,0:T(8,128)(2,1)} fusion(bf16[256,64,40]{0,2,1:T(8,128)(2,1)S(1)} %copy.23, bf16[64,40,4096]{2,1,0:T(8,128)(2,1)} %bitcast.38), kind=kOutput, calls=%fused_computation.22 | convolution fusion | flops 5369757696 | bytes 24379392 | tf_op jit(solution)/abtec,aebcd->abtd/dot_general | solution.py:8
  722.9 0.0 copy-done.1
  (1 shorter events, 0.0 us)
Async XLA Ops:
  0.0 11.7 %copy-start = (bf16[1,1,256,4096]{3,2,1,0:T(8,128)(2,1)S(1)}, bf16[1,1,256,4096]{3,2,1,0:T(8,128)(2,1)}, u32[]{:S(2)}) copy-start(bf16[1,1,256,4096]{3,2,1,0:T(8,128)(2,1)} %param.3) | copy-start | bytes 6291460
  1.0 0.9 copy-start.2
  1.8 0.7 copy-start.4
  428.6 5.1 copy-start.6
  428.6 5.2 copy-start.3
  428.6 5.2 copy-start.5
  428.6 282.9 %all-to-all-start.1 = ((bf16[1,2,32,1,40,4096]{5,4,1,3,0,2:T(8,128)(2,1)}), bf16[1,2,32,1,40,4096]{5,4,1,3,0,2:T(8,128)(2,1)}, u32[]{:S(2)}, u32[]{:S(2)}) async-start(bf16[1,2,32,1,40,4096]{5,4,1,3,0,2:T(8,128)(2,1)} %copy.16), calls=%async_computation.1 | async-start | bytes 41943040 | tf_op jit(solution)/sharding_constraint;jit(solution)/sharding_constraint | solution.py:13
  433.9 289.1 %copy-start.1 = (bf16[1,1,256,4096]{3,2,1,0:T(8,128)(2,1)S(1)}, bf16[1,1,256,4096]{3,2,1,0:T(8,128)(2,1)}, u32[]{:S(2)}) copy-start(bf16[1,1,256,4096]{3,2,1,0:T(8,128)(2,1)} %param.3) | copy-start | bytes 6291460
where the time goes:
time: 735 us; the launch traced here: 723 us
  waiting for transfers between devices  268 us (36%)
  blocking collectives  259 us (35%)
  matrix products  159 us (22%)
  local copies, waits for them, and re-layouts  31.3 us (4%)
    another operation x1, waiting for transfers between devices, placed(): return lax.with_sharding_constraint(v, NamedSharding(mesh, P(*spec)))  268 us
    another operation x1, blocking collectives, placed(): return lax.with_sharding_constraint(v, NamedSharding(mesh, P(*spec)))  259 us
    dot_general x7, matrix products, einsum(): return jnp.einsum(form, a.astype(jnp.float32), b.astype(jnp.float32))  159 us
    another operation x1, local copies, waits for them, and re-layouts, placed(): return lax.with_sharding_constraint(v, NamedSharding(mesh, P(*spec)))  17.5 us
  transfers between devices with their start and end apart: 1, of which 1 were waited for; matrix products, arithmetic and copies ran while one was open for 1% of the time, Pallas kernels for 0%

commit v1 on v0

v1 whole, which is shorter than its diff:
```python
import functools

import jax
import jax.numpy as jnp
from jax import lax
from jax.experimental import pallas as pl
from jax.experimental.pallas import tpu as pltpu
from jax.sharding import PartitionSpec as P

MESH = pl.DeviceIdType.MESH
F32, BF16 = jnp.float32, jnp.bfloat16
HC = 256
NT = 512
KINDS = ((0, 0), (0, -1), (0, 1), (-1, 0), (-1, 1), (1, 0), (1, -1))
ROWS = (-1, 0, 1)
TWO = range(2)
SIG = (1, -1)
FP, FM, SP, SM, HERE = (1, 0), (-1, 0), (0, 1), (0, -1), (0, 0)
OTHER, FAR = 1, 2
rem, div = lax.rem, lax.div


def kind(r, d):
    return KINDS.index((r, d))


def place(n):
    me = lax.axis_index("ep")
    c, chip = rem(me, 2), div(me, 2)
    a, b = div(chip, n), rem(chip, n)
    f, s = a * (1 - c) + b * c, b * (1 - c) + a * c

    def chip_at(at):
        ff, ss = rem(f + at[0] + n, n), rem(s + at[1] + n, n)
        return (ff * (1 - c) + ss * c) * n + ss * (1 - c) + ff * c

    def dev(at, other=0):
        return {"ep": chip_at(at) * 2 + (1 - c if other else c)}

    return dev, chip_at


def signal(sem, device):
    pl.semaphore_signal(sem, inc=1, device_id=device, device_id_type=MESH)


def greet(devices):
    barrier = pltpu.get_barrier_semaphore()
    for d in devices:
        signal(barrier, d)
    pl.semaphore_wait(barrier, len(devices))


def times(s, at=SP):
    return tuple(s * v for v in at)


def columns(j, h):
    return pl.ds(pl.multiple_of((2 * j + h) * HC, HC), HC)


def dot(a, b):
    return jnp.dot(a, b, preferred_element_type=F32)


def up_kernel(
    n, chunks, top, x_ref, meta_ref, lid_ref, wg_ref, wu_ref, h_ref, near_ref,
    row, nxt, zbuf, leaf, rel, part, p_ref, metas, wbuf, acc, hst, send, recv, msend, mrecv, msem, xsem, wsem, hsem, cred,
):
    dev, chip_at = place(n)
    c40 = p_ref.shape[2] // 4
    w = n * c40
    partner = dev(HERE, OTHER)
    sources = [(df, ds) for df in range(n) for ds in ROWS if (df, ds) != HERE]
    greet([dev(at) for at in sources] + [dev(at, OTHER) for at in (FP, FM, SP, SM)] + [partner])

    def remote(src, dst, s, r, to):
        return pltpu.make_async_remote_copy(
            src_ref=src, dst_ref=dst, send_sem=s, recv_sem=r, device_id=to, device_id_type=MESH
        )

    def copy(i, j, src, dst, to):
        m = rem(j, 3)
        return remote(src, dst, send.at[m, i], recv.at[m, i], to)

    tell = [
        remote(meta_ref, metas.at[-df % n, 1 - ds], msend.at[i], mrecv.at[i], dev((df, ds)))
        for i, (df, ds) in enumerate(sources)
    ]
    own = pltpu.make_async_copy(meta_ref, metas.at[0, 1], msem.at[0])

    def ring(j):
        r = row.at[rem(j, 3)]
        return [copy(h, j, r.at[:, 0], r.at[:, -SIG[h] % n], dev(times(SIG[h], FP))) for h in TWO]

    def onward(j):
        r = row.at[rem(j, 3)]
        return [copy(2 + h, j, r.at[h, -SIG[h] % n], r.at[h, FAR], dev(times(SIG[h], FP))) for h in TWO]

    def raw(j):
        r, t = row.at[rem(j, 3)], nxt.at[rem(j, 2)]
        return [copy(4 + h, j, r.at[h], t.at[h], dev(times(SIG[h]))) for h in TWO]

    def leaves(j, h):
        z, q = zbuf.at[rem(j, 3)], leaf.at[rem(j, 2)]
        return [copy(6 + 2 * h + o, j, q.at[h, o], z.at[h, o, SIG[h] % n], dev(times(-SIG[h]), o)) for o in TWO]

    def relays(j, h):
        z, q = zbuf.at[rem(j, 3)], rel.at[rem(j, 2)]
        return [copy(10 + 2 * h + o, j, q.at[h, o], z.at[h, o, FAR], dev(times(SIG[h]), o)) for o in TWO]

    def mine(j):
        z, q = zbuf.at[rem(j, 3)], part.at[rem(j, 2)]
        return copy(14, j, q.at[0], z.at[:, 1, 0], partner)

    def mine_next(j, h):
        z, q = zbuf.at[rem(j, 3)], part.at[rem(j, 2)]
        return copy(15 + h, j, q.at[1, h], z.at[h, 1, -SIG[h] % n], partner)

    def load(j):
        r, s = row.at[rem(j, 3)], xsem.at[rem(j, 2)]
        return [pltpu.make_async_copy(x_ref.at[:, columns(j, h)], r.at[h, 0], s.at[h]) for h in TWO]

    def weights(i, m, e):
        rows = pl.ds(pl.multiple_of(i * 2 * HC, HC), 2 * HC)
        return pltpu.make_async_copy((wg_ref, wu_ref)[m].at[e, rows], wbuf.at[m, e], wsem.at[m, e])

    def into_slots(k, src, put):
        for pair in TWO:
            r = [dot(p_ref[k, 2 * pair + i], src[2 * pair + i]) for i in TWO]
            for o in TWO:
                for e in TWO:
                    cut = slice((2 * o + e) * c40, (2 * o + e + 1) * c40)
                    v = jnp.concatenate([r[0][cut], r[1][cut]], axis=0).astype(BF16)
                    put(o, e, pl.ds(2 * pair * c40, 2 * c40), v)

    def matmul(i, m, e):
        weights(i, m, e).wait()
        tiles = acc.shape[-1] // NT
        z = zbuf.at[rem(i, 3)]

        def tile(t, carry):
            side, cols = div(t, tiles), pl.ds(pl.multiple_of(rem(t, tiles) * NT, NT), NT)
            a = jnp.concatenate([z[h, side, :, e].reshape(n * w, HC) for h in TWO], axis=1)
            acc[m, e, side, :, cols] += dot(a, wbuf[m, e, :, cols])
            return carry

        lax.fori_loop(0, 2 * tiles, tile, 0)

        @pl.when(i + 1 < chunks)
        def _():
            weights(i + 1, m, e).start()

    for d in load(0) + [own] + tell:
        d.start()
    for m in TWO:
        for e in TWO:
            weights(0, m, e).start()

    def tables():
        own.wait()
        for d in tell:
            d.wait_recv()
        lid = lid_ref[...]

        def source(g, carry):
            for k, (r, d) in enumerate(KINDS):
                first = (chip_at((0, d)) * 4 * c40).astype(F32)
                hit = None
                for j in range(top):
                    same = (metas[g, 1 + r, j : j + 1, :] - first) == lid
                    hit = same if hit is None else hit | same
                p_ref[k, g] = jnp.where(hit, 1.0, 0.0).astype(BF16)
            return carry

        lax.fori_loop(0, n, source, 0)
        for d in tell:
            d.wait_send()
        save = pltpu.make_async_copy(metas, near_ref, msem.at[1])
        save.start()
        acc[...] = jnp.zeros_like(acc)
        save.wait()

    def step(k, carry):
        @pl.when(k >= 2)
        def _():
            for i in range(7):
                pl.semaphore_wait(cred.at[i], 1)

        @pl.when(k < chunks)
        def _():
            for d in load(k):
                d.wait()
            for d in ring(k):
                d.start()

        @pl.when(k + 1 < chunks)
        def _():
            for d in load(k + 1):
                d.start()

        j, i = k - 1, k - 2
        travels, multiplies = (k >= 1) & (k <= chunks), k >= 2

        @pl.when(travels)
        def _():
            for d in onward(j):
                d.wait_recv()
            for d in raw(j):
                d.start()
            m3, m2 = rem(j, 3), rem(j, 2)
            for h in TWO:

                def put(o, e, rows, v):
                    leaf[m2, h, o, e, rows, :] = v

                into_slots(kind(0, -SIG[h]), row.at[m3, h], put)
                for d in leaves(j, h):
                    d.start()
            for h in TWO:

                def put(o, e, rows, v):
                    if o == 0:
                        zbuf[m3, h, 0, 0, e, rows, :] = v
                    else:
                        part[m2, 0, h, e, rows, :] = v

                into_slots(kind(*HERE), row.at[m3, h], put)
            mine(j).start()

        @pl.when(k == 0)
        def _():
            tables()

        @pl.when(multiplies)
        def _():
            for h in TWO:
                for d in leaves(i, h) + relays(i, h) + [mine_next(i, h)]:
                    d.wait_recv()
            mine(i).wait_recv()
            matmul(i, 0, 0)

        @pl.when(k < chunks)
        def _():
            for d, e in zip(ring(k), onward(k)):
                d.wait_recv()
                e.start()

        @pl.when(multiplies)
        def _():
            matmul(i, 0, 1)

        @pl.when(travels)
        def _():
            m3, m2 = rem(j, 3), rem(j, 2)
            for h in TWO:
                raw(j)[h].wait_recv()

                def put(o, e, rows, v):
                    rel[m2, h, o, e, rows, :] = v

                into_slots(kind(-SIG[h], SIG[h]), nxt.at[m2, h], put)
                for d in relays(j, h):
                    d.start()
            for h in TWO:

                def put(o, e, rows, v):
                    if o == 0:
                        zbuf[m3, h, 0, -SIG[h] % n, e, rows, :] = v
                    else:
                        part[m2, 1, h, e, rows, :] = v

                into_slots(kind(-SIG[h], 0), nxt.at[m2, h], put)
                mine_next(j, h).start()

        @pl.when(multiplies)
        def _():
            for e in TWO:
                matmul(i, 1, e)

        @pl.when(travels)
        def _():
            for d in ring(j) + onward(j) + raw(j) + leaves(j, 0) + leaves(j, 1) + [mine(j)]:
                d.wait_send()

        @pl.when(multiplies)
        def _():
            for h in TWO:
                for d in relays(i, h) + [mine_next(i, h)]:
                    d.wait_send()

        @pl.when(k < chunks)
        def _():
            to = [dev(at) for at in (FM, FP, SM, SP)] + [dev(at, OTHER) for at in (FM, FP)] + [partner]
            for q, d in enumerate(to):
                signal(cred.at[q], d)

        return carry

    lax.fori_loop(0, chunks + 2, step, 0)

    def save(t):
        e, side, soff = div(t, 2 * n), div(rem(t, 2 * n), n), rem(t, n)
        return pltpu.make_async_copy(hst.at[rem(t, 2)], h_ref.at[e, side, soff], hsem.at[rem(t, 2)])

    blocks = 4 * n

    def gated(t, carry):
        e, side, soff = div(t, 2 * n), div(rem(t, 2 * n), n), rem(t, n)
        rows = pl.ds(pl.multiple_of(soff * w, w), w)

        @pl.when(t >= 2)
        def _():
            save(t - 2).wait()

        hst[rem(t, 2)] = (jax.nn.silu(acc[0, e, side, rows, :]) * acc[1, e, side, rows, :]).astype(BF16)
        save(t).start()
        return carry

    lax.fori_loop(0, blocks, gated, 0)
    for t in (blocks - 2, blocks - 1):
        save(t).wait()


def down_kernel(
    n, chunks, top, h_ref, wd_ref, metas, lid_ref, y_ref,
    hbuf, wbuf, c_ref, ob, orl, olf, opt, yrow, f2r, fr, yst, fst, fin, ysum, y0, yo, send, recv, wsem, hsem, ysem, cred,
):
    dev, chip_at = place(n)
    rows2 = c_ref.shape[3] // 4
    w = hbuf.shape[3]
    partner = dev(HERE, OTHER)
    greet([dev(at, o) for at in (FP, FM, SP, SM) for o in TWO] + [partner])

    def m4(j):
        return rem(j, 4)

    def copy(i, j, src, dst, to):
        m = m4(j)
        return pltpu.make_async_remote_copy(
            src_ref=src, dst_ref=dst, send_sem=send.at[m, i], recv_sem=recv.at[m, i], device_id=to, device_id_type=MESH
        )

    def to_relay(j, h):
        o, q = ob.at[m4(j)], orl.at[m4(j)]
        to = dev(times(-SIG[h])), dev(times(-SIG[h], FP), OTHER)
        return [copy(2 * v + h, j, o.at[h, v, FAR], q.at[h, v], to[v]) for v in TWO]

    def to_root(j, h):
        o, q = ob.at[m4(j)], olf.at[m4(j)]
        to = dev(times(SIG[h])), dev(times(SIG[h], FP), OTHER)
        return [copy(4 + 2 * v + h, j, o.at[h, v, SIG[h] % n], q.at[h, v], to[v]) for v in TWO]

    def mine(j, h):
        o, q = ob.at[m4(j)], opt.at[m4(j)]
        ends = ((0, 8 + h, 0), (1, 10 + h, -SIG[h] % n))
        return [copy(i, j, o.at[h, 1, s], q.at[v, h], partner) for v, i, s in ends]

    def relayed(j):
        return [copy(12 + h, j, yst.at[rem(j, 2), h], yrow.at[m4(j), h], dev(times(-SIG[h]))) for h in TWO]

    def far(j):
        return [copy(14 + h, j, fst.at[rem(j, 2), h], f2r.at[m4(j), h], dev(times(-SIG[h], FP))) for h in TWO]

    def near(j):
        return [copy(16 + h, j, fin.at[rem(j, 2), h], fr.at[m4(j), h], dev(times(-SIG[h], FP))) for h in TWO]

    def firsts(j):
        return [d for h in TWO for d in to_relay(j, h) + to_root(j, h) + mine(j, h)]

    def weights(j):
        b, s = wbuf.at[rem(j, 2)], wsem.at[rem(j, 2)]
        return [pltpu.make_async_copy(wd_ref.at[e, :, columns(j, h)], b.at[h, e], s.at[h, e]) for h in TWO for e in TWO]

    def save(j):
        b = yo.at[rem(j, 2)]
        return [pltpu.make_async_copy(b.at[h], y_ref.at[:, columns(j, h)], ysem.at[h]) for h in TWO]

    def hidden(e, side):
        return pltpu.make_async_copy(h_ref.at[e, side], hbuf.at[e, side], hsem.at[e, side])

    def tokens(k, g, ours, theirs):
        cut = pl.ds((g // 2) * rows2, rows2)
        v = jnp.concatenate([o[e, cut, :] for o in (ours, theirs) for e in TWO], axis=0)
        return dot(c_ref[k, g], v)

    for side in TWO:
        for e in TWO:
            hidden(e, side).start()
    for d in weights(0):
        d.start()

    def tables():
        def source(g, carry):
            lid = lid_ref[rem(g, 2)]
            for r in ROWS:
                meta = metas[g, 1 + r].T
                for d in ROWS:
                    if (r, d) in KINDS:
                        first = (chip_at((0, d)) * 2 * rows2).astype(F32)
                        v = jnp.zeros(c_ref.shape[2:], F32)
                        for j in range(top):
                            same = (meta[:, j : j + 1] - first) == lid
                            v = jnp.where(same, meta[:, top + j : top + j + 1], v)
                        c_ref[kind(r, d), g] = v.astype(BF16)
            return carry

        lax.fori_loop(0, n, source, 0)

    def step(k, carry):
        @pl.when(k >= 2)
        def _():
            for i in range(7):
                pl.semaphore_wait(cred.at[i], 1)

        @pl.when((k >= 2) & (k <= chunks + 1))
        def _():
            j = k - 2
            m, m2 = m4(j), rem(j, 2)
            for d in to_root(j, 0) + to_root(j, 1) + [mine(j, h)[0] for h in TWO] + relayed(j):
                d.wait_recv()
            for h in TWO:
                s = SIG[h]
                for g in (2, 1, 3, 0):
                    v = tokens(kind(*HERE), g, ob.at[m, h, 0, 0], opt.at[m, 0, h])
                    v += tokens(kind(0, -s), g, olf.at[m, h, 0], olf.at[m, h, 1])
                    v += yrow[m, h, g].astype(F32)
                    if g == FAR:
                        fst[m2, h] = v.astype(BF16)
                        far(j)[h].start()
                    elif g == 0:
                        y0[m2, h] = v
                    else:
                        ysum[h, g // 2] = v

        @pl.when((k >= 1) & (k <= chunks))
        def _():
            j = k - 1
            m = m4(j)
            for h in TWO:
                s = SIG[h]
                for d in to_relay(j, h) + mine(j, h)[1:]:
                    d.wait_recv()
                for g in range(n):
                    v = tokens(kind(-s, 0), g, ob.at[m, h, 0, -s % n], opt.at[m, 1, h])
                    v += tokens(kind(-s, s), g, orl.at[m, h, 0], orl.at[m, h, 1])
                    yst[rem(j, 2), h, g] = v.astype(BF16)
                relayed(j)[h].start()

        @pl.when(k + 1 < chunks)
        def _():
            for d in weights(k + 1):
                d.start()

        @pl.when(k < chunks)
        def _():
            for d in weights(k):
                d.wait()
            m = m4(k)
            for h in TWO:
                for side in TWO:
                    for e in TWO:
                        if h == 0:

                            @pl.when(k == 0)
                            def _():
                                hidden(e, side).wait()

                        a = hbuf[e, side].reshape(n * w, hbuf.shape[4])
                        v = dot(a, wbuf[rem(k, 2), h, e]).astype(BF16)
                        ob[m, h, side, :, e] = v.reshape(n, w, HC)
                    to_relay(k, h)[side].start()
                    to_root(k, h)[side].start()
                for d in mine(k, h):
                    d.start()

        @pl.when(k == 0)
        def _():
            tables()

        @pl.when(k >= 3)
        def _():
            j = k - 3
            m, m2 = m4(j), rem(j, 2)
            for d in near(j):
                d.wait_recv()
            for h in TWO:
                yo[m2, h] = (y0[m2, h] + fr[m, 0, h].astype(F32) + fr[m, 1, h].astype(F32)).astype(BF16)
            for d in save(j):
                d.start()

        @pl.when((k >= 2) & (k <= chunks + 1))
        def _():
            j = k - 2
            m, m2 = m4(j), rem(j, 2)
            for h in TWO:
                far(j)[h].wait_recv()
                g = 1 - h
                fin[m2, h, h] = (ysum[h, g] + f2r[m, h].astype(F32)).astype(BF16)
                fin[m2, h, 1 - h] = ysum[1 - h, g].astype(BF16)
                near(j)[h].start()

        @pl.when((k >= 1) & (k <= chunks))
        def _():
            for d in firsts(k - 1):
                d.wait_send()

        @pl.when((k >= 2) & (k <= chunks + 1))
        def _():
            for d in relayed(k - 2):
                d.wait_send()

        @pl.when(k >= 3)
        def _():
            for d in far(k - 3) + near(k - 3):
                d.wait_send()
            for d in save(k - 3):
                d.wait()

        @pl.when(k < chunks + 1)
        def _():
            to = [dev(at) for at in (FM, FP, SM, SP)] + [dev(at, OTHER) for at in (SM, SP)] + [partner]
            for q, d in enumerate(to):
                signal(cred.at[q], d)

        return carry

    lax.fori_loop(0, chunks + 3, step, 0)


ANY = pl.BlockSpec(memory_space=pl.ANY)
VMEM = pl.BlockSpec(memory_space=pltpu.VMEM)
DMA, REGULAR = pltpu.SemaphoreType.DMA, pltpu.SemaphoreType.REGULAR


def bf16(*shape):
    return pltpu.VMEM(shape, BF16)


def f32(*shape):
    return pltpu.VMEM(shape, F32)


def params(i):
    return pltpu.CompilerParams(collective_id=i, has_side_effects=True, vmem_limit_bytes=66_500_000)


def up(n, slots, top, x, meta, lid, wg, wu):
    t, d = x.shape
    w, ff = n * slots, wg.shape[-1]
    slot_rows = bf16(2, 2, 2, 2, w, HC)
    return pl.pallas_call(
        functools.partial(up_kernel, n, d // (2 * HC), top),
        out_shape=(
            jax.ShapeDtypeStruct((2, 2, n, w, ff), BF16),
            jax.ShapeDtypeStruct((n, len(ROWS), *meta.shape), F32),
        ),
        in_specs=[ANY, VMEM, VMEM, ANY, ANY],
        out_specs=(ANY, ANY),
        scratch_shapes=[
            bf16(3, 2, n, t, HC),
            bf16(2, 2, n, t, HC),
            bf16(3, 2, 2, n, 2, w, HC),
            slot_rows,
            slot_rows,
            slot_rows,
            bf16(len(KINDS), n, 4 * slots, t),
            f32(n, len(ROWS), *meta.shape),
            bf16(2, 2, 2 * HC, ff),
            f32(2, 2, 2, n * w, ff),
            bf16(2, w, ff),
            DMA((3, 17)),
            DMA((3, 17)),
            DMA((3 * n - 1,)),
            DMA((3 * n - 1,)),
            DMA((2,)),
            DMA((2, 2)),
            DMA((2, 2)),
            DMA((2,)),
            REGULAR((7,)),
        ],
        compiler_params=params(0),
        name="up",
    )(x, meta, lid, wg, wu)


def down(n, slots, top, h, wd, metas, lid):
    d = wd.shape[-1]
    t, w, ff = metas.shape[-1], n * slots, h.shape[-1]
    rows = bf16(4, 2, 2, 2, w, HC)
    return pl.pallas_call(
        functools.partial(down_kernel, n, d // (2 * HC), top),
        out_shape=jax.ShapeDtypeStruct((t, d), BF16),
        in_specs=[ANY, ANY, VMEM, VMEM],
        out_specs=ANY,
        scratch_shapes=[
            bf16(2, 2, n, w, ff),
            bf16(2, 2, 2, ff, HC),
            bf16(len(KINDS), n, t, 8 * slots),
            bf16(4, 2, 2, n, 2, w, HC),
            rows,
            rows,
            rows,
            bf16(4, 2, n, t, HC),
            bf16(4, 2, t, HC),
            bf16(4, 2, 2, t, HC),
            bf16(2, 2, n, t, HC),
            bf16(2, 2, t, HC),
            bf16(2, 2, 2, t, HC),
            f32(2, 2, t, HC),
            f32(2, 2, t, HC),
            bf16(2, 2, t, HC),
            DMA((4, 18)),
            DMA((4, 18)),
            DMA((2, 2, 2)),
            DMA((2, 2)),
            DMA((2,)),
            REGULAR((7,)),
        ],
        compiler_params=params(1),
        name="down",
    )(h, wd, metas, lid)


def solution(mesh):
    n = round((mesh.shape["ep"] // 2) ** 0.5)

    def local(x, expert, slot, gate, w_gate, w_up, w_down):
        tokens, top = expert.shape[2:]
        experts = w_gate.shape[0] * mesh.shape["ep"]
        slots = 5 * tokens * top // (4 * experts)
        key = jnp.where(slot < slots, expert * slots + slot, -1)
        meta = jnp.concatenate([key[0, 0].T.astype(F32), gate[0, 0].T.astype(BF16).astype(F32)])
        c = rem(lax.axis_index("ep"), 2)
        lid = jnp.arange(4 * slots).reshape(2, 2, 1, slots)
        lid = jnp.where(c == 0, lid, lid[::-1]).astype(F32)
        up_lid = jnp.broadcast_to(lid.reshape(-1, 1), (4 * slots, tokens))
        none = jnp.full_like(lid, -experts * slots * 2)
        down_lid = jnp.stack([jnp.concatenate([lid, none], 2), jnp.concatenate([none, lid], 2)]).reshape(2, 1, -1)
        h, metas = up(n, slots, top, x[0, 0], meta, up_lid, w_gate, w_up)
        return down(n, slots, top, h, w_down, metas, down_lid)[None, None]

    tok, exp = P("dp", "ep", None, None), P("ep", None, None)
    return jax.shard_map(
        local, mesh=mesh, in_specs=(tok, tok, tok, tok, exp, exp, exp), out_specs=tok, check_vma=False
    )
```

time: 735 us -> 381 us (0.52); the launches traced: 723 us -> 380 us
  Pallas kernels: 0 us -> 372 us
  waiting for transfers between devices: 268 us -> 0 us
  blocking collectives: 259 us -> 0 us
  matrix products: 159 us -> 0 us
  local copies, waits for them, and re-layouts: 31.3 us -> 4.65 us
    pallas_call x0 -> x2, Pallas kernels: none -> 372 us  [the longest x1 191 us: up(): pl.pallas_call(functools.partial(up_kernel, n, d // (2 * HC), top), out_s...]
    another operation x1 -> x0, waiting for transfers between devices: 268 us -> none  [placed(): return lax.with_sharding_constraint(v, NamedSharding(mesh, P(*spec)))]
    another operation x1 -> x0, blocking collectives: 259 us -> none  [placed(): return lax.with_sharding_constraint(v, NamedSharding(mesh, P(*spec)))]
    dot_general x7 -> x0, matrix products: 159 us -> none  [einsum(): return jnp.einsum(form, a.astype(jnp.float32), b.astype(jnp.float32))]
    another operation x1 -> x2, local copies, waits for them, and re-layouts: 17.5 us -> 0.16 us  [local(): jnp.stack([jnp.concatenate([lid, none], 2), jnp.concatenate([none, lid],...]
    convert_element_type x3 -> x1, local copies, waits for them, and re-layouts: 11.4 us -> 0.51 us  [local(): lid = jnp.where(c == 0, lid, lid[::-1]).astype(F32)]
  transfers between devices with their start and end apart: 1 -> 0, of which waited for: 1 -> 0; matrix products, arithmetic and copies ran while one was open for 1% -> 0% of each run, Pallas kernels for 0% -> 0%
where the time goes in v1:
time: 381 us; the launch traced here: 380 us
  Pallas kernels  372 us (98%)
  local copies, waits for them, and re-layouts  4.65 us (1%)
    pallas_call x1, Pallas kernels, up(): pl.pallas_call(functools.partial(up_kernel, n, d // (2 * HC), top), out_s...  191 us
    pallas_call x1, Pallas kernels, down(): pl.pallas_call(functools.partial(down_kernel, n, d // (2 * HC), top), out...  181 us

profile of v1, /device:TPU:98, one launch (start us, length us, event | category | flops | bytes accessed | tf_op | source)
XLA Modules:
  0.0 379.8 jit_solution(11531670503438842346)
XLA Ops:
  0.0 0.5 broadcast.38
  0.5 0.7 fusion.1
  1.2 0.1 broadcast_in_dim.16
  1.3 0.7 convert_bitcast_fusion.1
  2.0 0.7 convert_bitcast_fusion
  2.7 0.6 pad_maximum_fusion.meta_ref
  3.3 0.1 stack.9
  3.4 0.1 stack.10
  3.5 0.6 pad_maximum_fusion.1.lid_ref
  4.1 0.8 broadcast_in_dim.17.lid_ref
  4.8 191.2 %up.1 = (bf16[2,2,4,160,1536]{4,3,2,1,0:T(8,128)(2,1)}, f32[4,3,16,256]{3,2,1,0:T(8,128)}) custom-call(bf16[256,4096]{1,0:T(8,128)(2,1)} %bitcast.12, f32[16,256]{1,0:T(8,128)} %pad_maximum_fusion.meta_ref, f32[160,256]{1,0:T(8,128)} %broadcast_in_dim.17.lid_ref, bf16[2,4096,1536]{2,1,0:T(8,128)(2,1)} %wg_ref.1, bf16[2,4096,1536]{2,1,0:T(8,128)(2,1)} %wu_ref.1), custom_call_target="tpu_custom_call" | custom-call | tf_op jit(solution)/shard_map/up/pallas_call | solution.py:552
  196.0 180.7 %down.1 = bf16[256,4096]{1,0:T(8,128)(2,1)} custom-call(bf16[2,2,4,160,1536]{4,3,2,1,0:T(8,128)(2,1)} %get-tuple-element.7.h_ref, bf16[2,1536,4096]{2,1,0:T(8,128)(2,1)} %wd_ref.1, f32[4,3,16,256]{3,2,1,0:T(8,128)} %get-tuple-element.8.metas, f32[2,1,320]{2,1,0:T(1,128)} %pad_maximum_fusion.1.lid_ref), custom_call_target="tpu_custom_call" | custom-call | tf_op jit(solution)/shard_map/down/pallas_call | solution.py:591
  376.7 3.1 copy.9
  (2 shorter events, 0.0 us)

commit v2 on v1

--- a/solution.py
+++ b/solution.py
@@ -9,10 +9,10 @@
 
 MESH = pl.DeviceIdType.MESH
 F32, BF16 = jnp.float32, jnp.bfloat16
-HC = 256
-NT = 512
+UP, DOWN = 256, 256
 KINDS = ((0, 0), (0, -1), (0, 1), (-1, 0), (-1, 1), (1, 0), (1, -1))
 ROWS = (-1, 0, 1)
+ROWS3 = (1, 2, 3)
 TWO = range(2)
 SIG = (1, -1)
 FP, FM, SP, SM, HERE = (1, 0), (-1, 0), (0, 1), (0, -1), (0, 0)
@@ -37,7 +37,7 @@
     def dev(at, other=0):
         return {"ep": chip_at(at) * 2 + (1 - c if other else c)}
 
-    return dev, chip_at
+    return dev, chip_at, c
 
 
 def signal(sem, device):
@@ -55,8 +55,8 @@
     return tuple(s * v for v in at)
 
 
-def columns(j, h):
-    return pl.ds(pl.multiple_of((2 * j + h) * HC, HC), HC)
+def columns(j, h, width):
+    return pl.ds(pl.multiple_of((2 * j + h) * width, width), width)
 
 
 def dot(a, b):
@@ -64,10 +64,10 @@
 
 
 def up_kernel(
-    n, chunks, top, x_ref, meta_ref, lid_ref, wg_ref, wu_ref, h_ref, near_ref,
+    n, chunks, top, x_ref, meta_ref, wg_ref, wu_ref, h_ref, near_ref,
     row, nxt, zbuf, leaf, rel, part, p_ref, metas, wbuf, acc, hst, send, recv, msend, mrecv, msem, xsem, wsem, hsem, cred,
 ):
-    dev, chip_at = place(n)
+    dev, chip_at, core = place(n)
     c40 = p_ref.shape[2] // 4
     w = n * c40
     partner = dev(HERE, OTHER)
@@ -98,7 +98,7 @@
         return [copy(2 + h, j, r.at[h, -SIG[h] % n], r.at[h, FAR], dev(times(SIG[h], FP))) for h in TWO]
 
     def raw(j):
-        r, t = row.at[rem(j, 3)], nxt.at[rem(j, 2)]
+        r, t = row.at[rem(j, 3)], nxt.at[rem(j, 3)]
         return [copy(4 + h, j, r.at[h], t.at[h], dev(times(SIG[h]))) for h in TWO]
 
     def leaves(j, h):
@@ -119,33 +119,28 @@
 
     def load(j):
         r, s = row.at[rem(j, 3)], xsem.at[rem(j, 2)]
-        return [pltpu.make_async_copy(x_ref.at[:, columns(j, h)], r.at[h, 0], s.at[h]) for h in TWO]
+        return [pltpu.make_async_copy(x_ref.at[:, columns(j, h, UP)], r.at[h, 0], s.at[h]) for h in TWO]
 
     def weights(i, m, e):
-        rows = pl.ds(pl.multiple_of(i * 2 * HC, HC), 2 * HC)
+        rows = pl.ds(pl.multiple_of(i * 2 * UP, UP), 2 * UP)
         return pltpu.make_async_copy((wg_ref, wu_ref)[m].at[e, rows], wbuf.at[m, e], wsem.at[m, e])
 
-    def into_slots(k, src, put):
+    def into_slots(kinds, src, puts):
         for pair in TWO:
-            r = [dot(p_ref[k, 2 * pair + i], src[2 * pair + i]) for i in TWO]
-            for o in TWO:
-                for e in TWO:
-                    cut = slice((2 * o + e) * c40, (2 * o + e + 1) * c40)
-                    v = jnp.concatenate([r[0][cut], r[1][cut]], axis=0).astype(BF16)
-                    put(o, e, pl.ds(2 * pair * c40, 2 * c40), v)
+            many = [jnp.concatenate([p_ref[k, 2 * pair + i] for k in kinds], axis=0) for i in TWO]
+            r = [dot(many[i], src[2 * pair + i]) for i in TWO]
+            for q, put in enumerate(puts):
+                for o in TWO:
+                    for e in TWO:
+                        at = (4 * q + 2 * o + e) * c40
+                        v = jnp.concatenate([x[at : at + c40] for x in r], axis=0).astype(BF16)
+                        put(o, e, pl.ds(2 * pair * c40, 2 * c40), v)
 
     def matmul(i, m, e):
         weights(i, m, e).wait()
-        tiles = acc.shape[-1] // NT
         z = zbuf.at[rem(i, 3)]
-
-        def tile(t, carry):
-            side, cols = div(t, tiles), pl.ds(pl.multiple_of(rem(t, tiles) * NT, NT), NT)
-            a = jnp.concatenate([z[h, side, :, e].reshape(n * w, HC) for h in TWO], axis=1)
-            acc[m, e, side, :, cols] += dot(a, wbuf[m, e, :, cols])
-            return carry
-
-        lax.fori_loop(0, 2 * tiles, tile, 0)
+        a = jnp.concatenate([z[h, :, :, e].reshape(2 * n * w, UP) for h in TWO], axis=1)
+        acc[m, e] += dot(a, wbuf[m, e]).reshape(acc.shape[2:])
 
         @pl.when(i + 1 < chunks)
         def _():
@@ -161,7 +156,9 @@
         own.wait()
         for d in tell:
             d.wait_recv()
-        lid = lid_ref[...]
+        at = lax.broadcasted_iota(jnp.int32, p_ref.shape[2:], 0)
+        swap = jnp.where(at < 2 * c40, 2 * c40, -2 * c40)
+        lid = (at + swap * core).astype(F32)
 
         def source(g, carry):
             for k, (r, d) in enumerate(KINDS):
@@ -178,7 +175,6 @@
             d.wait_send()
         save = pltpu.make_async_copy(metas, near_ref, msem.at[1])
         save.start()
-        acc[...] = jnp.zeros_like(acc)
         save.wait()
 
     def step(k, carry):
@@ -204,33 +200,31 @@
 
         @pl.when(travels)
         def _():
-            for d in onward(j):
-                d.wait_recv()
-            for d in raw(j):
-                d.start()
+
+            @pl.when(k == 1)
+            def _():
+                tables()
+
             m3, m2 = rem(j, 3), rem(j, 2)
             for h in TWO:
 
-                def put(o, e, rows, v):
+                def out(o, e, rows, v):
                     leaf[m2, h, o, e, rows, :] = v
 
-                into_slots(kind(0, -SIG[h]), row.at[m3, h], put)
-                for d in leaves(j, h):
-                    d.start()
-            for h in TWO:
-
-                def put(o, e, rows, v):
+                def keep(o, e, rows, v):
                     if o == 0:
                         zbuf[m3, h, 0, 0, e, rows, :] = v
                     else:
                         part[m2, 0, h, e, rows, :] = v
 
-                into_slots(kind(*HERE), row.at[m3, h], put)
+                into_slots((kind(0, -SIG[h]), kind(*HERE)), row.at[m3, h], (out, keep))
+                for d in leaves(j, h):
+                    d.start()
             mine(j).start()
 
-        @pl.when(k == 0)
-        def _():
-            tables()
+        @pl.when(k == 1)
+        def _():
+            acc[...] = jnp.zeros_like(acc)
 
         @pl.when(multiplies)
         def _():
@@ -256,22 +250,26 @@
             for h in TWO:
                 raw(j)[h].wait_recv()
 
-                def put(o, e, rows, v):
+                def out(o, e, rows, v):
                     rel[m2, h, o, e, rows, :] = v
 
-                into_slots(kind(-SIG[h], SIG[h]), nxt.at[m2, h], put)
-                for d in relays(j, h):
-                    d.start()
-            for h in TWO:
-
-                def put(o, e, rows, v):
+                def keep(o, e, rows, v):
                     if o == 0:
                         zbuf[m3, h, 0, -SIG[h] % n, e, rows, :] = v
                     else:
                         part[m2, 1, h, e, rows, :] = v
 
-                into_slots(kind(-SIG[h], 0), nxt.at[m2, h], put)
+                into_slots((kind(-SIG[h], SIG[h]), kind(-SIG[h], 0)), nxt.at[m3, h], (out, keep))
+                for d in relays(j, h):
+                    d.start()
                 mine_next(j, h).start()
+
+        @pl.when(k < chunks)
+        def _():
+            for d in onward(k):
+                d.wait_recv()
+            for d in raw(k):
+                d.start()
 
         @pl.when(multiplies)
         def _():
@@ -323,10 +321,10 @@
 
 
 def down_kernel(
-    n, chunks, top, h_ref, wd_ref, metas, lid_ref, y_ref,
+    n, chunks, top, h_ref, wd_ref, metas, y_ref,
     hbuf, wbuf, c_ref, ob, orl, olf, opt, yrow, f2r, fr, yst, fst, fin, ysum, y0, yo, send, recv, wsem, hsem, ysem, cred,
 ):
-    dev, chip_at = place(n)
+    dev, chip_at, core = place(n)
     rows2 = c_ref.shape[3] // 4
     w = hbuf.shape[3]
     partner = dev(HERE, OTHER)
@@ -370,19 +368,21 @@
 
     def weights(j):
         b, s = wbuf.at[rem(j, 2)], wsem.at[rem(j, 2)]
-        return [pltpu.make_async_copy(wd_ref.at[e, :, columns(j, h)], b.at[h, e], s.at[h, e]) for h in TWO for e in TWO]
+        cols = pl.ds(pl.multiple_of(2 * j * DOWN, DOWN), 2 * DOWN)
+        return [pltpu.make_async_copy(wd_ref.at[e, :, cols], b.at[e], s.at[e]) for e in TWO]
 
     def save(j):
         b = yo.at[rem(j, 2)]
-        return [pltpu.make_async_copy(b.at[h], y_ref.at[:, columns(j, h)], ysem.at[h]) for h in TWO]
+        return [pltpu.make_async_copy(b.at[h], y_ref.at[:, columns(j, h, DOWN)], ysem.at[h]) for h in TWO]
 
     def hidden(e, side):
         return pltpu.make_async_copy(h_ref.at[e, side], hbuf.at[e, side], hsem.at[e, side])
 
-    def tokens(k, g, ours, theirs):
-        cut = pl.ds((g // 2) * rows2, rows2)
+    def tokens(k, pair, ours, theirs):
+        cut = pl.ds(pair * rows2, rows2)
         v = jnp.concatenate([o[e, cut, :] for o in (ours, theirs) for e in TWO], axis=0)
-        return dot(c_ref[k, g], v)
+        t = c_ref.shape[2]
+        return dot(c_ref[k, 2 * pair : 2 * pair + 2].reshape(2 * t, c_ref.shape[3]), v).reshape(2, t, DOWN)
 
     for side in TWO:
         for e in TWO:
@@ -391,8 +391,15 @@
         d.start()
 
     def tables():
+        at = lax.broadcasted_iota(jnp.int32, (1, c_ref.shape[3]), 1)
+        q = sum((at >= rows2 * i).astype(jnp.int32) for i in ROWS3)
+        at -= q * rows2
+        second = (at >= rows2 // 2).astype(jnp.int32)
+        slot = at - second * (rows2 // 2)
+        expert = q + jnp.where(q < 2, 2, -2) * core
+
         def source(g, carry):
-            lid = lid_ref[rem(g, 2)]
+            lid = jnp.where(second == rem(g, 2), expert * (rows2 // 2) + slot, -(2**20)).astype(F32)
             for r in ROWS:
                 meta = metas[g, 1 + r].T
                 for d in ROWS:
@@ -413,6 +420,17 @@
             for i in range(7):
                 pl.semaphore_wait(cred.at[i], 1)
 
+        @pl.when((k >= 3) & (k <= chunks + 2))
+        def _():
+            j = k - 3
+            m, m2 = m4(j), rem(j, 2)
+            for h in TWO:
+                far(j)[h].wait_recv()
+                g = 1 - h
+                fin[m2, h, h] = (ysum[m2, h, g] + f2r[m, h].astype(F32)).astype(BF16)
+                fin[m2, h, 1 - h] = ysum[m2, 1 - h, g].astype(BF16)
+                near(j)[h].start()
+
         @pl.when((k >= 2) & (k <= chunks + 1))
         def _():
             j = k - 2
@@ -421,17 +439,16 @@
                 d.wait_recv()
             for h in TWO:
                 s = SIG[h]
-                for g in (2, 1, 3, 0):
-                    v = tokens(kind(*HERE), g, ob.at[m, h, 0, 0], opt.at[m, 0, h])
-                    v += tokens(kind(0, -s), g, olf.at[m, h, 0], olf.at[m, h, 1])
-                    v += yrow[m, h, g].astype(F32)
-                    if g == FAR:
-                        fst[m2, h] = v.astype(BF16)
+                for pair in (1, 0):
+                    v = tokens(kind(*HERE), pair, ob.at[m, h, 0, 0], opt.at[m, 0, h])
+                    v += tokens(kind(0, -s), pair, olf.at[m, h, 0], olf.at[m, h, 1])
+                    v += yrow[m, h, 2 * pair : 2 * pair + 2].astype(F32)
+                    ysum[m2, h, pair] = v[1]
+                    if pair:
+                        fst[m2, h] = v[0].astype(BF16)
                         far(j)[h].start()
-                    elif g == 0:
-                        y0[m2, h] = v
                     else:
-                        ysum[h, g // 2] = v
+                        y0[m, h] = v[0]
 
         @pl.when((k >= 1) & (k <= chunks))
         def _():
@@ -441,10 +458,10 @@
                 s = SIG[h]
                 for d in to_relay(j, h) + mine(j, h)[1:]:
                     d.wait_recv()
-                for g in range(n):
-                    v = tokens(kind(-s, 0), g, ob.at[m, h, 0, -s % n], opt.at[m, 1, h])
-                    v += tokens(kind(-s, s), g, orl.at[m, h, 0], orl.at[m, h, 1])
-                    yst[rem(j, 2), h, g] = v.astype(BF16)
+                for pair in TWO:
+                    v = tokens(kind(-s, 0), pair, ob.at[m, h, 0, -s % n], opt.at[m, 1, h])
+                    v += tokens(kind(-s, s), pair, orl.at[m, h, 0], orl.at[m, h, 1])
+                    yst[rem(j, 2), h, 2 * pair : 2 * pair + 2] = v.astype(BF16)
                 relayed(j)[h].start()
 
         @pl.when(k + 1 < chunks)
@@ -457,20 +474,21 @@
             for d in weights(k):
                 d.wait()
             m = m4(k)
-            for h in TWO:
-                for side in TWO:
-                    for e in TWO:
-                        if h == 0:
-
-                            @pl.when(k == 0)
-                            def _():
-                                hidden(e, side).wait()
-
-                        a = hbuf[e, side].reshape(n * w, hbuf.shape[4])
-                        v = dot(a, wbuf[rem(k, 2), h, e]).astype(BF16)
-                        ob[m, h, side, :, e] = v.reshape(n, w, HC)
+            for side in TWO:
+                for e in TWO:
+
+                    @pl.when(k == 0)
+                    def _():
+                        hidden(e, side).wait()
+
+                    a = hbuf[e, side].reshape(n * w, hbuf.shape[4])
+                    v = dot(a, wbuf[rem(k, 2), e]).astype(BF16)
+                    for h in TWO:
+                        ob[m, h, side, :, e] = v[:, h * DOWN : (h + 1) * DOWN].reshape(n, w, DOWN)
+                for h in TWO:
                     to_relay(k, h)[side].start()
                     to_root(k, h)[side].start()
+            for h in TWO:
                 for d in mine(k, h):
                     d.start()
 
@@ -478,28 +496,17 @@
         def _():
             tables()
 
-        @pl.when(k >= 3)
-        def _():
-            j = k - 3
+        @pl.when(k >= 4)
+        def _():
+            j = k - 4
             m, m2 = m4(j), rem(j, 2)
             for d in near(j):
                 d.wait_recv()
             for h in TWO:
-                yo[m2, h] = (y0[m2, h] + fr[m, 0, h].astype(F32) + fr[m, 1, h].astype(F32)).astype(BF16)
+                yo[m2, h] = (y0[m, h] + fr[m, 0, h].astype(F32) + fr[m, 1, h].astype(F32)).astype(BF16)
             for d in save(j):
                 d.start()
 
-        @pl.when((k >= 2) & (k <= chunks + 1))
-        def _():
-            j = k - 2
-            m, m2 = m4(j), rem(j, 2)
-            for h in TWO:
-                far(j)[h].wait_recv()
-                g = 1 - h
-                fin[m2, h, h] = (ysum[h, g] + f2r[m, h].astype(F32)).astype(BF16)
-                fin[m2, h, 1 - h] = ysum[1 - h, g].astype(BF16)
-                near(j)[h].start()
-
         @pl.when((k >= 1) & (k <= chunks))
         def _():
             for d in firsts(k - 1):
@@ -510,14 +517,19 @@
             for d in relayed(k - 2):
                 d.wait_send()
 
-        @pl.when(k >= 3)
-        def _():
-            for d in far(k - 3) + near(k - 3):
+        @pl.when((k >= 3) & (k <= chunks + 2))
+        def _():
+            for d in far(k - 3):
                 d.wait_send()
-            for d in save(k - 3):
+
+        @pl.when(k >= 4)
+        def _():
+            for d in near(k - 4):
+                d.wait_send()
+            for d in save(k - 4):
                 d.wait()
 
-        @pl.when(k < chunks + 1)
+        @pl.when(k < chunks + 2)
         def _():
             to = [dev(at) for at in (FM, FP, SM, SP)] + [dev(at, OTHER) for at in (SM, SP)] + [partner]
             for q, d in enumerate(to):
@@ -525,7 +537,7 @@
 
         return carry
 
-    lax.fori_loop(0, chunks + 3, step, 0)
+    lax.fori_loop(0, chunks + 4, step, 0)
 
 
 ANY = pl.BlockSpec(memory_space=pl.ANY)
@@ -545,28 +557,28 @@
     return pltpu.CompilerParams(collective_id=i, has_side_effects=True, vmem_limit_bytes=66_500_000)
 
 
-def up(n, slots, top, x, meta, lid, wg, wu):
+def up(n, slots, top, x, meta, wg, wu):
     t, d = x.shape
     w, ff = n * slots, wg.shape[-1]
-    slot_rows = bf16(2, 2, 2, 2, w, HC)
+    slot_rows = bf16(2, 2, 2, 2, w, UP)
     return pl.pallas_call(
-        functools.partial(up_kernel, n, d // (2 * HC), top),
+        functools.partial(up_kernel, n, d // (2 * UP), top),
         out_shape=(
             jax.ShapeDtypeStruct((2, 2, n, w, ff), BF16),
             jax.ShapeDtypeStruct((n, len(ROWS), *meta.shape), F32),
         ),
-        in_specs=[ANY, VMEM, VMEM, ANY, ANY],
+        in_specs=[ANY, VMEM, ANY, ANY],
         out_specs=(ANY, ANY),
         scratch_shapes=[
-            bf16(3, 2, n, t, HC),
-            bf16(2, 2, n, t, HC),
-            bf16(3, 2, 2, n, 2, w, HC),
+            bf16(3, 2, n, t, UP),
+            bf16(3, 2, n, t, UP),
+            bf16(3, 2, 2, n, 2, w, UP),
             slot_rows,
             slot_rows,
             slot_rows,
             bf16(len(KINDS), n, 4 * slots, t),
             f32(n, len(ROWS), *meta.shape),
-            bf16(2, 2, 2 * HC, ff),
+            bf16(2, 2, 2 * UP, ff),
             f32(2, 2, 2, n * w, ff),
             bf16(2, w, ff),
             DMA((3, 17)),
@@ -581,45 +593,45 @@
         ],
         compiler_params=params(0),
         name="up",
-    )(x, meta, lid, wg, wu)
-
-
-def down(n, slots, top, h, wd, metas, lid):
+    )(x, meta, wg, wu)
+
+
+def down(n, slots, top, h, wd, metas):
     d = wd.shape[-1]
     t, w, ff = metas.shape[-1], n * slots, h.shape[-1]
-    rows = bf16(4, 2, 2, 2, w, HC)
+    rows = bf16(4, 2, 2, 2, w, DOWN)
     return pl.pallas_call(
-        functools.partial(down_kernel, n, d // (2 * HC), top),
+        functools.partial(down_kernel, n, d // (2 * DOWN), top),
         out_shape=jax.ShapeDtypeStruct((t, d), BF16),
-        in_specs=[ANY, ANY, VMEM, VMEM],
+        in_specs=[ANY, ANY, VMEM],
         out_specs=ANY,
         scratch_shapes=[
             bf16(2, 2, n, w, ff),
-            bf16(2, 2, 2, ff, HC),
+            bf16(2, 2, ff, 2 * DOWN),
             bf16(len(KINDS), n, t, 8 * slots),
-            bf16(4, 2, 2, n, 2, w, HC),
+            bf16(4, 2, 2, n, 2, w, DOWN),
             rows,
             rows,
             rows,
-            bf16(4, 2, n, t, HC),
-            bf16(4, 2, t, HC),
-            bf16(4, 2, 2, t, HC),
-            bf16(2, 2, n, t, HC),
-            bf16(2, 2, t, HC),
-            bf16(2, 2, 2, t, HC),
-            f32(2, 2, t, HC),
-            f32(2, 2, t, HC),
-            bf16(2, 2, t, HC),
+            bf16(4, 2, n, t, DOWN),
+            bf16(4, 2, t, DOWN),
+            bf16(4, 2, 2, t, DOWN),
+            bf16(2, 2, n, t, DOWN),
+            bf16(2, 2, t, DOWN),
+            bf16(2, 2, 2, t, DOWN),
+            f32(2, 2, 2, t, DOWN),
+            f32(4, 2, t, DOWN),
+            bf16(2, 2, t, DOWN),
             DMA((4, 18)),
             DMA((4, 18)),
-            DMA((2, 2, 2)),
+            DMA((2, 2)),
             DMA((2, 2)),
             DMA((2,)),
             REGULAR((7,)),
         ],
         compiler_params=params(1),
         name="down",
-    )(h, wd, metas, lid)
+    )(h, wd, metas)
 
 
 def solution(mesh):
@@ -631,14 +643,8 @@
         slots = 5 * tokens * top // (4 * experts)
         key = jnp.where(slot < slots, expert * slots + slot, -1)
         meta = jnp.concatenate([key[0, 0].T.astype(F32), gate[0, 0].T.astype(BF16).astype(F32)])
-        c = rem(lax.axis_index("ep"), 2)
-        lid = jnp.arange(4 * slots).reshape(2, 2, 1, slots)
-        lid = jnp.where(c == 0, lid, lid[::-1]).astype(F32)
-        up_lid = jnp.broadcast_to(lid.reshape(-1, 1), (4 * slots, tokens))
-        none = jnp.full_like(lid, -experts * slots * 2)
-        down_lid = jnp.stack([jnp.concatenate([lid, none], 2), jnp.concatenate([none, lid], 2)]).reshape(2, 1, -1)
-        h, metas = up(n, slots, top, x[0, 0], meta, up_lid, w_gate, w_up)
-        return down(n, slots, top, h, w_down, metas, down_lid)[None, None]
+        h, metas = up(n, slots, top, x[0, 0], meta, w_gate, w_up)
+        return down(n, slots, top, h, w_down, metas)[None, None]
 
     tok, exp = P("dp", "ep", None, None), P("ep", None, None)
     return jax.shard_map(

time: 381 us -> 360 us (0.945)
  Pallas kernels: 372 us -> 354 us
    pallas_call x2, Pallas kernels: 372 us -> 354 us  [the longest x1 180 us: down(): pl.pallas_call(functools.partial(down_kernel, n, d // (2 * DOWN), top), o...]
where the time goes in v2:
time: 360 us
  Pallas kernels  354 us (98%)
    pallas_call x1, Pallas kernels, down(): pl.pallas_call(functools.partial(down_kernel, n, d // (2 * DOWN), top), o...  180 us
    pallas_call x1, Pallas kernels, up(): pl.pallas_call(functools.partial(up_kernel, n, d // (2 * UP), top), out_s...  174 us

profile of v2, /device:TPU:98, one launch (start us, length us, event | category | flops | bytes accessed | tf_op | source)
XLA Modules:
  0.0 359.6 jit_solution(4050705969197249443)
XLA Ops:
  0.0 0.7 convert_bitcast_fusion.1
  0.7 0.7 convert_bitcast_fusion
  1.4 0.6 pad_maximum_fusion.meta_ref
  2.0 174.2 %up.1 = (bf16[2,2,4,160,1536]{4,3,2,1,0:T(8,128)(2,1)}, f32[4,3,16,256]{3,2,1,0:T(8,128)}) custom-call(bf16[256,4096]{1,0:T(8,128)(2,1)} %bitcast.12, f32[16,256]{1,0:T(8,128)} %pad_maximum_fusion.meta_ref, bf16[2,4096,1536]{2,1,0:T(8,128)(2,1)} %wg_ref.1, bf16[2,4096,1536]{2,1,0:T(8,128)(2,1)} %wu_ref.1), custom_call_target="tpu_custom_call" | custom-call | tf_op jit(solution)/shard_map/up/pallas_call | solution.py:564
  176.2 180.2 %down.1 = bf16[256,4096]{1,0:T(8,128)(2,1)} custom-call(bf16[2,2,4,160,1536]{4,3,2,1,0:T(8,128)(2,1)} %get-tuple-element.7.h_ref, bf16[2,1536,4096]{2,1,0:T(8,128)(2,1)} %wd_ref.1, f32[4,3,16,256]{3,2,1,0:T(8,128)} %get-tuple-element.8.metas), custom_call_target="tpu_custom_call" | custom-call | tf_op jit(solution)/shard_map/down/pallas_call | solution.py:603
  356.4 3.1 copy.9

commit v3 on v2

--- a/solution.py
+++ b/solution.py
@@ -390,7 +390,7 @@
     for d in weights(0):
         d.start()
 
-    def tables():
+    def tables(sources):
         at = lax.broadcasted_iota(jnp.int32, (1, c_ref.shape[3]), 1)
         q = sum((at >= rows2 * i).astype(jnp.int32) for i in ROWS3)
         at -= q * rows2
@@ -400,7 +400,7 @@
 
         def source(g, carry):
             lid = jnp.where(second == rem(g, 2), expert * (rows2 // 2) + slot, -(2**20)).astype(F32)
-            for r in ROWS:
+            for r in sources:
                 meta = metas[g, 1 + r].T
                 for d in ROWS:
                     if (r, d) in KINDS:
@@ -494,7 +494,11 @@
 
         @pl.when(k == 0)
         def _():
-            tables()
+            tables(SIG)
+
+        @pl.when(k == 1)
+        def _():
+            tables((0,))
 
         @pl.when(k >= 4)
         def _():

time: 360 us -> 355 us (0.986)
  Pallas kernels: 354 us -> 349 us
    pallas_call x1, Pallas kernels: 180 us -> 175 us  [down(): pl.pallas_call(functools.partial(down_kernel, n, d // (2 * DOWN), top), o...]
where the time goes in v3:
time: 355 us
  Pallas kernels  349 us (98%)
    pallas_call x1, Pallas kernels, down(): pl.pallas_call(functools.partial(down_kernel, n, d // (2 * DOWN), top), o...  175 us
    pallas_call x1, Pallas kernels, up(): pl.pallas_call(functools.partial(up_kernel, n, d // (2 * UP), top), out_s...  174 us

profile of v3, /device:TPU:98, one launch (start us, length us, event | category | flops | bytes accessed | tf_op | source)
XLA Modules:
  0.0 354.6 jit_solution(16373914771784753175)
XLA Ops:
  0.0 0.7 convert_bitcast_fusion.1
  0.7 0.7 convert_bitcast_fusion
  1.4 0.6 pad_maximum_fusion.meta_ref
  2.0 174.2 %up.1 = (bf16[2,2,4,160,1536]{4,3,2,1,0:T(8,128)(2,1)}, f32[4,3,16,256]{3,2,1,0:T(8,128)}) custom-call(bf16[256,4096]{1,0:T(8,128)(2,1)} %bitcast.12, f32[16,256]{1,0:T(8,128)} %pad_maximum_fusion.meta_ref, bf16[2,4096,1536]{2,1,0:T(8,128)(2,1)} %wg_ref.1, bf16[2,4096,1536]{2,1,0:T(8,128)(2,1)} %wu_ref.1), custom_call_target="tpu_custom_call" | custom-call | tf_op jit(solution)/shard_map/up/pallas_call | solution.py:568
  176.2 175.2 %down.1 = bf16[256,4096]{1,0:T(8,128)(2,1)} custom-call(bf16[2,2,4,160,1536]{4,3,2,1,0:T(8,128)(2,1)} %get-tuple-element.7.h_ref, bf16[2,1536,4096]{2,1,0:T(8,128)(2,1)} %wd_ref.1, f32[4,3,16,256]{3,2,1,0:T(8,128)} %get-tuple-element.8.metas), custom_call_target="tpu_custom_call" | custom-call | tf_op jit(solution)/shard_map/down/pallas_call | solution.py:607
  351.5 3.1 copy.9
